TPU v7x, 32 devices: a whole 2x2x4 slice. The times are simulated.
32 devices in a mesh: blk: 16 (over z, y, x), auth: 2 (over core).
Axes of the slice: x: 2, y: 2, z: 4, core: 2. Of those that a mesh axis runs over, the one named last changes fastest.
Arguments:
- features: bfloat16 [2048, 1024], P('blk', 'auth'), may hold values from -6 to 6
- partners: int32 [16, 8], P('blk'), may hold values from 0 to 15, as said below
- tiles: bfloat16 [16, 8, 128, 128], P('blk'), may hold values from -0.125 to 0.125
- paper_w_in: bfloat16 [1024, 2048], P(None, 'auth'), may hold values from -0.1875 to 0.1875
- paper_w_out: bfloat16 [2048, 1024], P('auth'), may hold values from -0.125 to 0.125
- paper_gain: float32 [1024], replicated, may hold values from 0.5 to 1.5
- author_feats: bfloat16 [2048, 1024], P('blk', 'auth'), may hold values from -6 to 6
- assign: int32 [2048], P('blk'), may hold values from 0 to 127
- author_w_in: bfloat16 [1024, 2048], P(None, 'auth'), may hold values from -0.1875 to 0.1875
- author_w_out: bfloat16 [2048, 1024], P('auth'), may hold values from -0.125 to 0.125
- author_gain: float32 [1024], replicated, may hold values from 0.5 to 1.5
Outputs:
- paper_out: bfloat16 [2048, 1024], P('blk', 'auth')
- author_out: bfloat16 [2048, 1024], P('blk', 'auth')
Inputs may be any that keep to these rules, and one draw needn't show every extreme that they name: `partners`: each row names 8 different blocks and never its own; block c names block b exactly when block b names block c.
All inputs are finite; a program needn't handle non-finite values.
Results may differ from a plain program's by a relative error of at most 0.013.
Values may be sent and summed in bfloat16 or wider, within the bound.
A program may use at most 128 MiB of HBM per device.

v0:
```python
import functools

import jax
import jax.numpy as jnp
from jax import lax
from jax.experimental import pallas as pl
from jax.experimental.pallas import tpu as pltpu
from jax.sharding import PartitionSpec as P

epsilon = 1e-06
MESH = pl.DeviceIdType.MESH


def plane_dims(count):
    if count % 4 == 0 and count <= 32:
        return (count // 4, 2, 2)
    return None


def kernel(
    count,
    partners_ref,
    tiles_ref,
    feat_ref,
    p_in_hbm,
    p_out_hbm,
    p_gain_ref,
    afeat_ref,
    assign_ref,
    a_in_hbm,
    a_out_hbm,
    a_gain_ref,
    paper_out_ref,
    author_out_ref,
    w_p_in,
    w_p_out,
    w_a_in,
    w_a_out,
    dense,
    back,
    linked,
    mixed,
    pre,
    partial_send,
    partial_recv,
    afeat_other,
    apart_send,
    apart_recv,
    mid,
    w_sem,
    relay_send,
    relay_recv,
    tile_send,
    tile_recv,
    core_send,
    core_recv,
    gossip,
    total_ref,
):
    rows, width = feat_ref.shape
    half = rows // 2
    me = lax.axis_index("blk")
    core = lax.axis_index("auth")
    other = 1 - core
    slots = partners_ref.shape[1]

    weights = [
        pltpu.make_async_copy(source, target, w_sem.at[slot])
        for slot, (source, target) in enumerate(
            ((p_in_hbm, w_p_in), (p_out_hbm, w_p_out), (a_in_hbm, w_a_in), (a_out_hbm, w_a_out))
        )
    ]

    dims = plane_dims(count)
    barrier = pltpu.get_barrier_semaphore()

    def signal(semaphore, block):
        pl.semaphore_signal(semaphore, inc=1, device_id={"blk": block}, device_id_type=MESH)

    if dims is None:

        def greet(step, carry):
            signal(barrier, lax.rem(me + step, count))
            return carry

        lax.fori_loop(1, count, greet, 0)
        near = count - 1
    else:
        depth = dims[0]
        plane = 4
        z = me // plane
        y = lax.rem(me // 2, 2)
        x = lax.rem(me, 2)
        near = 2 + (z > 0).astype(jnp.int32) + (z < depth - 1).astype(jnp.int32)

        def signal_near(semaphore):
            signal(semaphore, me + 1 - 2 * x)
            signal(semaphore, me + 2 - 4 * y)
            pl.when(z > 0)(lambda: signal(semaphore, me - plane))
            pl.when(z < depth - 1)(lambda: signal(semaphore, me + plane))

        signal_near(barrier)
    pl.semaphore_signal(barrier, inc=1, device_id={"auth": other}, device_id_type=MESH)

    def fill(block, carry):
        index = jnp.int32(0)
        found = jnp.int32(0)
        for slot in range(slots):
            same = (partners_ref[0, slot] == block).astype(jnp.int32)
            index = jnp.maximum(index, same * slot)
            found = jnp.maximum(found, same)
        tile = tiles_ref[0, index].astype(jnp.float32) * found.astype(jnp.float32)
        tile = tile.astype(jnp.bfloat16)
        dense[0, block] = tile[:half]
        dense[1, block] = tile[half:]
        return carry

    linked[pl.ds(pl.multiple_of(me * rows, rows), rows), :] = feat_ref[...]
    back[core, me] = jnp.zeros((half, rows), jnp.bfloat16)

    pl.semaphore_wait(barrier, near + 1)

    def to_core(source, target, slot):
        return pltpu.make_async_remote_copy(
            src_ref=source,
            dst_ref=target,
            send_sem=core_send.at[slot],
            recv_sem=core_recv.at[slot],
            device_id={"auth": other},
            device_id_type=MESH,
        )

    def tile_copy(step):
        block = lax.rem(me + step, count)
        return pltpu.make_async_remote_copy(
            src_ref=dense.at[core, block],
            dst_ref=back.at[core, me],
            send_sem=tile_send.at[step],
            recv_sem=tile_recv.at[step],
            device_id={"blk": block},
            device_id_type=MESH,
        )

    def start_tiles():
        if dims is not None:
            signal_near(gossip.at[0])
        lax.fori_loop(0, count, fill, 0)
        if dims is not None:
            for turn in range(depth):
                pl.semaphore_wait(gossip.at[turn], near)
                if turn < depth - 1:
                    signal_near(gossip.at[turn + 1])

        def one(step, carry):
            tile_copy(step).start()
            return carry

        lax.fori_loop(1, count, one, 0)

    afeat_copy = to_core(afeat_ref, afeat_other, 0)
    back_copy = to_core(back.at[core], back.at[core], 1)

    def finish_tiles():
        def one(step, carry):
            tile_copy(step).wait()
            return carry

        lax.fori_loop(1, count, one, 0)
        back_copy.start()

    def mix_tiles():
        back_copy.wait()

        def one(block, carry):
            own = jnp.concatenate([dense[0, block], dense[1, block]], axis=0)
            came = jnp.concatenate([back[0, block], back[1, block]], axis=0)
            whole = own.astype(jnp.float32) + came.astype(jnp.float32).T
            mixed[:, pl.ds(pl.multiple_of(block * rows, rows), rows)] = whole.astype(jnp.bfloat16)
            return carry

        lax.fori_loop(0, count, one, 0)

    if dims is None:

        def direct(step):
            return pltpu.make_async_remote_copy(
                src_ref=feat_ref,
                dst_ref=linked.at[pl.ds(pl.multiple_of(me * rows, rows), rows)],
                send_sem=relay_send.at[step],
                recv_sem=relay_recv.at[step],
                device_id={"blk": lax.rem(me + step, count)},
                device_id_type=MESH,
            )

        def start_one(step, carry):
            direct(step).start()
            return carry

        def wait_one(step, carry):
            direct(step).wait()
            return carry

        lax.fori_loop(1, count, start_one, 0)
        start_tiles()
        afeat_copy.start()
        for weight in weights:
            weight.start()
        finish_tiles()
        mix_tiles()
        lax.fori_loop(1, count, wait_one, 0)
    else:
        KINDS = {"up": 0, "down": 1, "x": 2, "y": 3, "far": 4}

        def move(kind, level, part):
            if kind == "up":
                origin, target, arrive = (y, x), me + plane, "col"
            elif kind == "down":
                origin, target, arrive = (y, x), me - plane, "col"
            elif kind == "x":
                origin, target, arrive = (y, x), me + 1 - 2 * x, "x"
            elif kind == "y":
                origin, target, arrive = (y, x), me + 2 - 4 * y, "y"
            elif part == 0:
                origin, target, arrive = (y, 1 - x), me + 2 - 4 * y, "far"
            else:
                origin, target, arrive = (1 - y, x), me + 1 - 2 * x, "far"
            block = level * plane + origin[0] * 2 + origin[1]
            place = pl.ds(pl.multiple_of(block * rows + part * half, half), half)
            spot = (level * 2 + part) * 5
            return pltpu.make_async_remote_copy(
                src_ref=linked.at[place],
                dst_ref=linked.at[place],
                send_sem=relay_send.at[spot + KINDS[kind]],
                recv_sem=relay_recv.at[(level * 2 + part) * 4 + ("col", "x", "y", "far").index(arrive)],
                device_id={"blk": target},
                device_id_type=MESH,
            )

        def arrived(arrive, level, part):
            origin = {"col": (y, x), "x": (y, 1 - x), "y": (1 - y, x), "far": (1 - y, 1 - x)}[arrive]
            block = level * plane + origin[0] * 2 + origin[1]
            place = pl.ds(pl.multiple_of(block * rows + part * half, half), half)
            pltpu.make_async_copy(
                linked.at[place],
                linked.at[place],
                relay_recv.at[(level * 2 + part) * 4 + ("col", "x", "y", "far").index(arrive)],
            ).wait()

        def levels(distance):
            if distance == 0:
                return ((z, None),)
            return ((z - distance, z >= distance), (z + distance, z < depth - distance))

        def when(condition, body):
            if condition is None:
                body()
            else:
                pl.when(condition)(body)

        def column(distance):
            for part in range(2):
                for side, (level, valid) in enumerate(levels(distance)):

                    def body(level=level, side=side, part=part):
                        arrived("col", level, part)
                        if side == 0:
                            pl.when(z < depth - 1)(lambda: move("up", level, part).start())
                        else:
                            pl.when(z > 0)(lambda: move("down", level, part).start())
                        move("x", level, part).start()
                        move("y", level, part).start()

                    when(valid, body)

        def beside(distance):
            for level, valid in levels(distance):

                def body(level=level):
                    arrived("x", level, 0)
                    move("far", level, 0).start()
                    arrived("y", level, 1)
                    move("far", level, 1).start()

                when(valid, body)

        for part in range(2):
            pl.when(z < depth - 1)(lambda part=part: move("up", z, part).start())
            pl.when(z > 0)(lambda part=part: move("down", z, part).start())
            first, second = ("x", "y") if part == 0 else ("y", "x")
            move(first, z, part).start()
            move(second, z, part).start()
        afeat_copy.start()
        for weight in weights:
            weight.start()
        start_tiles()
        total_ref[...] = feat_ref[...].astype(jnp.float32)

        def gather(distance):
            for level, valid in levels(distance):

                def rest(level=level):
                    for arrive, part in (("x", 1), ("y", 0), ("far", 0), ("far", 1)):
                        arrived(arrive, level, part)
                    span = plane * rows
                    start = pl.multiple_of(level * span, span)
                    total_ref[...] += jnp.dot(
                        mixed[:, pl.ds(start, span)],
                        linked[pl.ds(start, span), :],
                        preferred_element_type=jnp.float32,
                    )

                when(valid, rest)

        for distance in range(1, depth + 1):
            if distance < depth:
                column(distance)
            beside(distance - 1)
            if distance == max(depth - 2, 1):
                finish_tiles()
            if distance == max(depth - 1, 1):
                mix_tiles()
                for earlier in range(depth - 2):
                    gather(earlier)
        for distance in range(max(depth - 2, 0), depth):
            gather(distance)

    if dims is None:
        span = min(count * rows, 2048)

        def product(step, total):
            start = pl.multiple_of(step * span, span)
            return total + jnp.dot(
                mixed[:, pl.ds(start, span)],
                linked[pl.ds(start, span), :],
                preferred_element_type=jnp.float32,
            )

        total = feat_ref[...].astype(jnp.float32)
        total = lax.fori_loop(0, count * rows // span, product, total)
    else:
        total = total_ref[...]
    pre[core] = total.astype(jnp.bfloat16)
    pre_copy = to_core(pre.at[core], pre.at[core], 2)
    pre_copy.start()

    member = assign_ref[...] == lax.broadcasted_iota(jnp.int32, (afeat_ref.shape[0], rows), 0)
    member_wide = member.astype(jnp.float32)
    counts = jnp.maximum(jnp.sum(member_wide, axis=1, keepdims=True), 1.0)
    member_matrix = member_wide.astype(jnp.bfloat16)

    def hidden_of(left, right, w_in, gain):
        left = left.astype(jnp.float32)
        right = right.astype(jnp.float32)
        square = jnp.sum(left * left, axis=-1, keepdims=True)
        square = square + jnp.sum(right * right, axis=-1, keepdims=True)
        scale = lax.rsqrt(square / (2 * width) + epsilon)
        left = (left * scale * gain[:, :width]).astype(jnp.bfloat16)
        right = (right * scale * gain[:, width:]).astype(jnp.bfloat16)
        normed = jnp.concatenate([left, right], axis=1)
        units = jnp.dot(normed, w_in[...], preferred_element_type=jnp.float32)
        return (units / (1.0 + jnp.exp(-units))).astype(jnp.bfloat16)

    weights[0].wait()

    def scaled_units(side):
        values = pre[side].astype(jnp.float32)
        columns = pl.ds(pl.multiple_of(side * width, width), width)
        weighed = (values * p_gain_ref[:, columns]).astype(jnp.bfloat16)
        units = jnp.dot(weighed, w_p_in[columns, :], preferred_element_type=jnp.float32)
        return units, jnp.sum(values * values, axis=-1, keepdims=True)

    own_units, own_square = scaled_units(core)
    pre_copy.wait()
    far_units, far_square = scaled_units(other)
    scale = lax.rsqrt((own_square + far_square) / (2 * width) + epsilon)
    units = (own_units + far_units) * scale
    hidden = (units / (1.0 + jnp.exp(-units))).astype(jnp.bfloat16)
    weights[1].wait()
    terms = []
    partial_copies = []
    for side in range(2):
        term = jnp.dot(
            hidden,
            w_p_out[:, side * width : (side + 1) * width],
            preferred_element_type=jnp.float32,
        )
        terms.append(term)
        partial_send[side] = term.astype(jnp.bfloat16)
        copy = to_core(partial_send.at[side], partial_recv.at[side], 3 + side)
        copy.start()
        partial_copies.append(copy)
    afeat_copy.wait()
    author_pre = []
    for side in range(2):
        partial_copies[side].wait()
        sum_of = pre[side].astype(jnp.float32) + (
            terms[side] + partial_recv[side].astype(jnp.float32)
        )
        mid_side = sum_of.astype(jnp.bfloat16)
        mid[side] = mid_side
        author_sum = jnp.dot(member_matrix, mid_side, preferred_element_type=jnp.float32)
        mine = (core == side).astype(jnp.float32)
        base = afeat_ref[...].astype(jnp.float32) * mine
        base = base + afeat_other[...].astype(jnp.float32) * (1.0 - mine)
        author_pre.append((base + author_sum / counts).astype(jnp.bfloat16))
    weights[2].wait()
    hidden = hidden_of(author_pre[0], author_pre[1], w_a_in, a_gain_ref[...])
    weights[3].wait()
    theirs = pl.ds(pl.multiple_of(other * width, width), width)
    ours = pl.ds(pl.multiple_of(core * width, width), width)
    apart_send[...] = jnp.dot(
        hidden, w_a_out[:, theirs], preferred_element_type=jnp.float32
    ).astype(jnp.bfloat16)
    apart_copy = to_core(apart_send, apart_recv, 5)
    apart_copy.start()
    term = jnp.dot(hidden, w_a_out[:, ours], preferred_element_type=jnp.float32)
    mine = (core == 0).astype(jnp.float32)
    own_pre = author_pre[0].astype(jnp.float32) * mine
    own_pre = own_pre + author_pre[1].astype(jnp.float32) * (1.0 - mine)
    apart_copy.wait()
    author_out = (own_pre + (term + apart_recv[...].astype(jnp.float32))).astype(jnp.bfloat16)
    author_out_ref[...] = author_out
    returned = lax.dot_general(
        member_matrix,
        author_out,
        (((0,), (0,)), ((), ())),
        preferred_element_type=jnp.float32,
    )
    paper_out_ref[...] = (mid[core].astype(jnp.float32) + returned).astype(jnp.bfloat16)

    if dims is not None:
        for distance in range(depth):
            for side, (level, valid) in enumerate(levels(distance)):

                def sent(level=level, side=side, distance=distance):
                    for part in range(2):
                        if distance == 0 or side == 0:
                            pl.when(z < depth - 1)(lambda part=part: move("up", level, part).wait_send())
                        if distance == 0 or side == 1:
                            pl.when(z > 0)(lambda part=part: move("down", level, part).wait_send())
                        for kind in ("x", "y", "far"):
                            move(kind, level, part).wait_send()

                when(valid, sent)


def local(
    features,
    partners,
    tiles,
    paper_w_in,
    paper_w_out,
    paper_gain,
    author_feats,
    assign,
    author_w_in,
    author_w_out,
    author_gain,
):
    count = lax.axis_size("blk")
    rows, width = features.shape
    half = rows // 2
    bf16 = jnp.bfloat16
    vmem = pl.BlockSpec(memory_space=pltpu.VMEM)
    hbm = pl.BlockSpec(memory_space=pl.ANY)
    smem = pl.BlockSpec(memory_space=pltpu.SMEM)
    dims = plane_dims(count)
    sends = count if dims is None else dims[0] * 10
    receives = count if dims is None else dims[0] * 8
    rounds = 1 if dims is None else dims[0]
    return pl.pallas_call(
        functools.partial(kernel, count),
        out_shape=(
            jax.ShapeDtypeStruct(features.shape, bf16),
            jax.ShapeDtypeStruct(author_feats.shape, bf16),
        ),
        in_specs=[smem, vmem, vmem, hbm, hbm, vmem, vmem, vmem, hbm, hbm, vmem],
        out_specs=(vmem, vmem),
        scratch_shapes=[
            pltpu.VMEM(paper_w_in.shape, bf16),
            pltpu.VMEM(paper_w_out.shape, bf16),
            pltpu.VMEM(author_w_in.shape, bf16),
            pltpu.VMEM(author_w_out.shape, bf16),
            pltpu.VMEM((2, count, half, rows), bf16),
            pltpu.VMEM((2, count, half, rows), bf16),
            pltpu.VMEM((count * rows, width), bf16),
            pltpu.VMEM((rows, count * rows), bf16),
            pltpu.VMEM((2, rows, width), bf16),
            pltpu.VMEM((2, rows, width), bf16),
            pltpu.VMEM((2, rows, width), bf16),
            pltpu.VMEM(author_feats.shape, bf16),
            pltpu.VMEM(author_feats.shape, bf16),
            pltpu.VMEM(author_feats.shape, bf16),
            pltpu.VMEM((2, rows, width), bf16),
            pltpu.SemaphoreType.DMA((4,)),
            pltpu.SemaphoreType.DMA((sends,)),
            pltpu.SemaphoreType.DMA((receives,)),
            pltpu.SemaphoreType.DMA((count,)),
            pltpu.SemaphoreType.DMA((count,)),
            pltpu.SemaphoreType.DMA((6,)),
            pltpu.SemaphoreType.DMA((6,)),
            pltpu.SemaphoreType.REGULAR((rounds,)),
            pltpu.VMEM((rows, width), jnp.float32),
        ],
        compiler_params=pltpu.CompilerParams(
            collective_id=0, has_side_effects=True, vmem_limit_bytes=56 * 1024 * 1024
        ),
    )(
        partners,
        tiles,
        features,
        paper_w_in,
        paper_w_out,
        paper_gain[None, :],
        author_feats,
        assign[None, :],
        author_w_in,
        author_w_out,
        author_gain[None, :],
    )


def solution(mesh):
    placed = (
        P("blk", "auth"),
        P("blk", None),
        P("blk", None, None, None),
        P(None, "auth"),
        P("auth", None),
        P(),
        P("blk", "auth"),
        P("blk"),
        P(None, "auth"),
        P("auth", None),
        P(),
    )
    return jax.shard_map(
        local,
        mesh=mesh,
        in_specs=placed,
        out_specs=(P("blk", "auth"), P("blk", "auth")),
        check_vma=False,
    )
```

profile of v0, /device:TPU:0, one launch (start us, length us, event | category | flops | bytes accessed | tf_op | source)
XLA Modules:
  0.0 41.8 jit_solution(667991888696287798)
XLA Ops:
  0.6 38.0 %shard_map.122 = (bf16[128,512]{1,0:T(8,128)(2,1)}, bf16[128,512]{1,0:T(8,128)(2,1)}) custom-call(s32[1,8]{1,0:T(1,128)} %partners_ref.1, bf16[1,8,128,128]{3,2,1,0:T(8,128)(2,1)} %tiles_ref.1, bf16[128,512]{1,0:T(8,128)(2,1)} %feat_ref.1, bf16[1024,1024]{1,0:T(8,128)(2,1)} %p_in_hbm.1, bf16[1024,1024]{1,0:T(8,128)(2,1)} %p_out_hbm.1, f32[1,1024]{1,0:T(1,128)} %bitcast.3, ...), custom_call_target="tpu_custom_call" | custom-call | tf_op jit(solution)/shard_map/pallas_call | solution.py:471
  38.6 1.6 %copy.15 = bf16[128,512]{1,0:T(8,128)(2,1)} copy(bf16[128,512]{1,0:T(8,128)(2,1)} %get-tuple-element.4) | data formatting | bytes 262144
  40.2 1.6 %copy.16 = bf16[128,512]{1,0:T(8,128)(2,1)} copy(bf16[128,512]{1,0:T(8,128)(2,1)} %get-tuple-element.5) | data formatting | bytes 262144
where the time goes:
time: 41.9 us; the launch traced here: 41.8 us
  Pallas kernels  38 us (91%)
  local copies, waits for them, and re-layouts  3.14 us (7%)
  between operations  0.64 us (2%)
    pallas_call x1, Pallas kernels, local(): pl.pallas_call(functools.partial(kernel, count), out_shape=(jax.ShapeDtyp...  38 us
    unnamed x2, local copies, waits for them, and re-layouts  3.14 us

commit v1 on v0

--- a/solution.py
+++ b/solution.py
@@ -30,8 +30,7 @@
     a_in_hbm,
     a_out_hbm,
     a_gain_ref,
-    paper_out_ref,
-    author_out_ref,
+    result_ref,
     w_p_in,
     w_p_out,
     w_a_in,
@@ -419,14 +418,14 @@
     own_pre = own_pre + author_pre[1].astype(jnp.float32) * (1.0 - mine)
     apart_copy.wait()
     author_out = (own_pre + (term + apart_recv[...].astype(jnp.float32))).astype(jnp.bfloat16)
-    author_out_ref[...] = author_out
+    result_ref[1] = author_out
     returned = lax.dot_general(
         member_matrix,
         author_out,
         (((0,), (0,)), ((), ())),
         preferred_element_type=jnp.float32,
     )
-    paper_out_ref[...] = (mid[core].astype(jnp.float32) + returned).astype(jnp.bfloat16)
+    result_ref[0] = (mid[core].astype(jnp.float32) + returned).astype(jnp.bfloat16)
 
     if dims is not None:
         for distance in range(depth):
@@ -468,14 +467,11 @@
     sends = count if dims is None else dims[0] * 10
     receives = count if dims is None else dims[0] * 8
     rounds = 1 if dims is None else dims[0]
-    return pl.pallas_call(
+    (result,) = pl.pallas_call(
         functools.partial(kernel, count),
-        out_shape=(
-            jax.ShapeDtypeStruct(features.shape, bf16),
-            jax.ShapeDtypeStruct(author_feats.shape, bf16),
-        ),
+        out_shape=(pltpu.VMEM((2,) + features.shape, bf16),),
         in_specs=[smem, vmem, vmem, hbm, hbm, vmem, vmem, vmem, hbm, hbm, vmem],
-        out_specs=(vmem, vmem),
+        out_specs=(vmem,),
         scratch_shapes=[
             pltpu.VMEM(paper_w_in.shape, bf16),
             pltpu.VMEM(paper_w_out.shape, bf16),
@@ -518,6 +514,7 @@
         author_w_out,
         author_gain[None, :],
     )
+    return result[0], result[1]
 
 
 def solution(mesh):

time: 41.9 us -> 38.8 us (0.926)
  local copies, waits for them, and re-layouts: 3.14 us -> 0.72 us
  Pallas kernels: 38 us -> 37.3 us
    unnamed x2 -> x0, local copies, waits for them, and re-layouts: 3.14 us -> none
    squeeze x0 -> x1, local copies, waits for them, and re-layouts: none -> 0.72 us  [local(): return (result[0], result[1])]
    pallas_call x1, Pallas kernels: 38 us -> 37.3 us  [local(): pl.pallas_call(functools.partial(kernel, count), out_shape=(pltpu.VMEM((2...]
where the time goes in v1:
time: 38.8 us; the launch traced here: 38.6 us
  Pallas kernels  37.3 us (96%)
  local copies, waits for them, and re-layouts  0.72 us (2%)
  between operations  0.64 us (2%)
    pallas_call x1, Pallas kernels, local(): pl.pallas_call(functools.partial(kernel, count), out_shape=(pltpu.VMEM((2...  37.3 us

profile of v1, /device:TPU:0, one launch (start us, length us, event | category | flops | bytes accessed | tf_op | source)
XLA Modules:
  0.0 38.6 jit_solution(3438625665226234508)
XLA Ops:
  0.6 37.3 %shard_map.122 = bf16[2,128,512]{2,1,0:T(8,128)(2,1)S(1)} custom-call(s32[1,8]{1,0:T(1,128)} %partners_ref.1, bf16[1,8,128,128]{3,2,1,0:T(8,128)(2,1)} %tiles_ref.1, bf16[128,512]{1,0:T(8,128)(2,1)} %feat_ref.1, bf16[1024,1024]{1,0:T(8,128)(2,1)} %p_in_hbm.1, bf16[1024,1024]{1,0:T(8,128)(2,1)} %p_out_hbm.1, f32[1,1024]{1,0:T(1,128)} %bitcast.7, ...), custom_call_target="tpu_custom_call" | custom-call | tf_op jit(solution)/shard_map/pallas_call | solution.py:470
  37.9 0.7 %slice_bitcast_fusion = (bf16[128,512]{1,0:T(8,128)(2,1)}, bf16[128,512]{1,0:T(8,128)(2,1)}) fusion(bf16[2,128,512]{2,1,0:T(8,128)(2,1)S(1)} %shard_map.122), kind=kLoop, calls=%fused_computation | loop fusion | bytes 524288 | tf_op jit(solution)/shard_map/squeeze | solution.py:517

commit v2 on v1

v2 whole, which is shorter than its diff:
```python
import functools

import jax
import jax.numpy as jnp
from jax import lax
from jax.experimental import pallas as pl
from jax.experimental.pallas import tpu as pltpu
from jax.sharding import PartitionSpec as P

epsilon = 1e-06
MESH = pl.DeviceIdType.MESH
LANES = 128
PLANE = 4
RING = 4


def to_other_core(source, target, send_sem, recv_sem, slot, other):
    return pltpu.make_async_remote_copy(
        src_ref=source,
        dst_ref=target,
        send_sem=send_sem.at[slot],
        recv_sem=recv_sem.at[slot],
        device_id={"auth": other},
        device_id_type=MESH,
    )


def membership(assign_ref, authors, rows):
    member = assign_ref[...] == lax.broadcasted_iota(jnp.int32, (authors, rows), 0)
    member_wide = member.astype(jnp.float32)
    counts = jnp.maximum(jnp.sum(member_wide, axis=1, keepdims=True), 1.0)
    return member_wide.astype(jnp.bfloat16), counts


def silu(units):
    return (units / (1.0 + jnp.exp(-units))).astype(jnp.bfloat16)


def scaled_units(pre, side, width, p_gain_ref, w_p_in):
    values = pre[side].astype(jnp.float32)
    columns = pl.ds(pl.multiple_of(side * width, width), width)
    weighed = (values * p_gain_ref[:, columns]).astype(jnp.bfloat16)
    units = jnp.dot(weighed, w_p_in[columns, :], preferred_element_type=jnp.float32)
    return units, jnp.sum(values * values, axis=-1, keepdims=True)


def after_hidden(
    core,
    hidden,
    member_matrix,
    counts,
    weights,
    to_core,
    slots,
    afeat,
    afeat_other,
    pre,
    w_p_out,
    w_a_in,
    w_a_out,
    a_gain_ref,
    partial_send,
    partial_recv,
    apart_send,
    apart_recv,
    mid,
    result_ref,
):
    other = 1 - core
    width = afeat.shape[1]
    weights[1].wait()
    terms = []
    partial_copies = []
    for side in range(2):
        term = jnp.dot(
            hidden,
            w_p_out[:, side * width : (side + 1) * width],
            preferred_element_type=jnp.float32,
        )
        terms.append(term)
        partial_send[side] = term.astype(jnp.bfloat16)
        copy = to_core(partial_send.at[side], partial_recv.at[side], slots[side])
        copy.start()
        partial_copies.append(copy)
    author_pre = []
    for side in range(2):
        partial_copies[side].wait()
        sum_of = pre[side].astype(jnp.float32) + (
            terms[side] + partial_recv[side].astype(jnp.float32)
        )
        mid_side = sum_of.astype(jnp.bfloat16)
        mid[side] = mid_side
        author_sum = jnp.dot(member_matrix, mid_side, preferred_element_type=jnp.float32)
        mine = (core == side).astype(jnp.float32)
        base = afeat[...].astype(jnp.float32) * mine
        base = base + afeat_other[...].astype(jnp.float32) * (1.0 - mine)
        author_pre.append((base + author_sum / counts).astype(jnp.bfloat16))
    weights[2].wait()
    left = author_pre[0].astype(jnp.float32)
    right = author_pre[1].astype(jnp.float32)
    square = jnp.sum(left * left, axis=-1, keepdims=True)
    square = square + jnp.sum(right * right, axis=-1, keepdims=True)
    scale = lax.rsqrt(square / (2 * width) + epsilon)
    gain = a_gain_ref[...]
    left = (left * scale * gain[:, :width]).astype(jnp.bfloat16)
    right = (right * scale * gain[:, width:]).astype(jnp.bfloat16)
    normed = jnp.concatenate([left, right], axis=1)
    hidden = silu(jnp.dot(normed, w_a_in[...], preferred_element_type=jnp.float32))
    weights[3].wait()
    theirs = pl.ds(pl.multiple_of(other * width, width), width)
    ours = pl.ds(pl.multiple_of(core * width, width), width)
    apart_send[...] = jnp.dot(
        hidden, w_a_out[:, theirs], preferred_element_type=jnp.float32
    ).astype(jnp.bfloat16)
    apart_copy = to_core(apart_send, apart_recv, slots[2])
    apart_copy.start()
    term = jnp.dot(hidden, w_a_out[:, ours], preferred_element_type=jnp.float32)
    mine = (core == 0).astype(jnp.float32)
    own_pre = author_pre[0].astype(jnp.float32) * mine
    own_pre = own_pre + author_pre[1].astype(jnp.float32) * (1.0 - mine)
    apart_copy.wait()
    author_out = (own_pre + (term + apart_recv[...].astype(jnp.float32))).astype(jnp.bfloat16)
    result_ref[1] = author_out
    returned = lax.dot_general(
        member_matrix,
        author_out,
        (((0,), (0,)), ((), ())),
        preferred_element_type=jnp.float32,
    )
    result_ref[0] = (mid[core].astype(jnp.float32) + returned).astype(jnp.bfloat16)


def grid_kernel(
    count,
    partners_ref,
    tiles_hbm,
    feat_hbm,
    p_in_hbm,
    p_out_hbm,
    p_gain_ref,
    afeat_hbm,
    assign_ref,
    a_in_hbm,
    a_out_hbm,
    a_gain_ref,
    result_ref,
    w_p_in,
    w_p_out,
    w_a_in,
    w_a_out,
    tiles,
    plane_tiles,
    ring_tiles,
    ahead,
    back,
    mixed,
    linked,
    product,
    part_send,
    part_recv,
    pre,
    partial_send,
    partial_recv,
    afeat,
    afeat_other,
    apart_send,
    apart_recv,
    mid,
    w_sem,
    load_sem,
    ring_send,
    ring_recv,
    tile_send,
    tile_recv,
    part_send_sem,
    part_recv_sem,
    core_send,
    core_recv,
):
    rows, width = afeat.shape
    half = rows // 2
    chunks = linked.shape[0]
    wide = width // chunks
    me = lax.axis_index("blk")
    core = lax.axis_index("auth")
    other = 1 - core
    slots = partners_ref.shape[1]
    z = me // PLANE
    y = lax.rem(me // 2, 2)
    x = lax.rem(me, 2)
    place = lax.rem(me, PLANE)

    def across(step):
        far_x = 1 - x if step % 2 else x
        far_y = 1 - y if step // 2 else y
        return far_y * 2 + far_x

    def level(step):
        return lax.rem(z + step, RING)

    def rows_of(index, size=rows):
        return pl.ds(pl.multiple_of(index * size, size), size)

    mine = rows_of(core, half)
    steps = range(1, PLANE)

    loads = [
        pltpu.make_async_copy(
            feat_hbm.at[:, n * wide : (n + 1) * wide],
            linked.at[n, rows_of(z)],
            load_sem.at[n],
        )
        for n in range(chunks)
    ]
    tile_load = pltpu.make_async_copy(tiles_hbm.at[0], tiles, load_sem.at[chunks])
    afeat_load = pltpu.make_async_copy(afeat_hbm, afeat, load_sem.at[chunks + 1])
    weights = [
        pltpu.make_async_copy(source, target, w_sem.at[slot])
        for slot, (source, target) in enumerate(
            ((p_in_hbm, w_p_in), (p_out_hbm, w_p_out), (a_in_hbm, w_a_in), (a_out_hbm, w_a_out))
        )
    ]

    barrier = pltpu.get_barrier_semaphore()
    for step in steps:
        for block in (z * PLANE + across(step), level(step) * PLANE + place):
            pl.semaphore_signal(barrier, inc=1, device_id={"blk": block}, device_id_type=MESH)
    pl.semaphore_signal(barrier, inc=1, device_id={"auth": other}, device_id_type=MESH)
    for load in loads:
        load.start()
    tile_load.start()
    afeat_load.start()

    def remote(source, target, send_sem, recv_sem, block):
        return pltpu.make_async_remote_copy(
            src_ref=source,
            dst_ref=target,
            send_sem=send_sem,
            recv_sem=recv_sem,
            device_id={"blk": block},
            device_id_type=MESH,
        )

    def arrived(target, semaphore):
        pltpu.make_async_copy(target, target, semaphore).wait()

    def to_core(source, target, slot):
        return to_other_core(source, target, core_send, core_recv, slot, other)

    even = 1 - lax.rem(z, 2)
    relay_from = lax.rem(z + 1 + 2 * even, RING)
    relay_to = lax.rem(z + 1 + 2 * (1 - even), RING)

    def ring_copy(kind, n):
        origin, target = (
            (z, level(1)),
            (z, level(RING - 1)),
            (relay_from, relay_to),
        )[kind]
        spot = linked.at[n, rows_of(origin)]
        return remote(
            spot,
            spot,
            ring_send.at[n * 3 + kind],
            ring_recv.at[n * RING + origin],
            target * PLANE + place,
        )

    def ring_arrived(n, origin):
        arrived(linked.at[n, rows_of(origin)], ring_recv.at[n * RING + origin])

    def plane_copy(step):
        return remote(
            plane_tiles.at[across(step), mine],
            ahead.at[place, mine],
            tile_send.at[step - 1],
            tile_recv.at[step - 1],
            z * PLANE + across(step),
        )

    def column_copy(step):
        return remote(
            ring_tiles.at[level(step), mine],
            back.at[z, mine],
            tile_send.at[PLANE + step - 1],
            tile_recv.at[PLANE + step - 1],
            level(step) * PLANE + place,
        )

    def part_copy(n, step):
        return remote(
            part_send.at[n, across(step)],
            part_recv.at[n, step - 1],
            part_send_sem.at[n * 3 + step - 1],
            part_recv_sem.at[n * 3 + step - 1],
            z * PLANE + across(step),
        )

    def start_own(n):
        ring_copy(0, n).start()
        ring_copy(1, n).start()

    def relay(n):
        ring_arrived(n, relay_from)
        ring_copy(2, n).start()

    for load in loads:
        load.wait()
    pl.semaphore_wait(barrier, 2 * (PLANE - 1) + 1)
    start_own(0)
    tile_load.wait()
    for block in range(count):
        index = jnp.int32(0)
        found = jnp.int32(0)
        for slot in range(slots):
            same = (partners_ref[0, slot] == block).astype(jnp.int32)
            index = jnp.maximum(index, same * slot)
            found = jnp.maximum(found, same)
        tile = tiles[index].astype(jnp.float32) * found.astype(jnp.float32)
        tile = tile.astype(jnp.bfloat16)
        upper, inner = block // PLANE, block % PLANE
        ring_tiles[upper, :, inner * rows : (inner + 1) * rows] = tile
        plane_tiles[inner, :, upper * rows : (upper + 1) * rows] = tile
    for step in (2, 1, 3):
        column_copy(step).start()
    for step in (3, 1, 2):
        plane_copy(step).start()
    start_own(1)
    for weight in weights:
        weight.start()
    afeat_load.wait()
    afeat_copy = to_core(afeat, afeat_other, 0)
    afeat_copy.start()

    relay(0)
    start_own(2)

    ahead[place] = plane_tiles[place]
    plane_exchange = []
    for step in steps:
        spot = ahead.at[across(step), mine]
        arrived(spot, tile_recv.at[step - 1])
        copy = to_core(spot, spot, step)
        copy.start()
        plane_exchange.append(copy)
    column_exchange = []
    for step in steps:
        spot = back.at[level(RING - step), mine]
        arrived(spot, tile_recv.at[PLANE + step - 1])
        copy = to_core(spot, spot, PLANE - 1 + step)
        copy.start()
        column_exchange.append(copy)
    relay(1)
    start_own(3)

    def mix(origin, came):
        columns = rows_of(origin)
        for inner in range(PLANE):
            own = ahead[inner, :, columns].astype(jnp.float32)
            there = came[origin, :, inner * rows : (inner + 1) * rows].astype(jnp.float32)
            mixed[inner * rows : (inner + 1) * rows, columns] = (own + there.T).astype(jnp.bfloat16)

    for copy in plane_exchange:
        copy.wait()
    mix(z, ring_tiles)
    for step in steps:
        column_exchange[step - 1].wait()
        mix(level(RING - step), back)

    def products(n):
        ring_arrived(n, relay_to)
        ring_arrived(n, level(2))
        total = jnp.dot(mixed[...], linked[n], preferred_element_type=jnp.float32)
        product[n] = total
        for inner in range(PLANE):
            part_send[n, inner] = total[inner * rows : (inner + 1) * rows].astype(jnp.bfloat16)
        for step in (3, 1, 2):
            part_copy(n, step).start()

    def collect(n):
        total = linked[n, rows_of(z)].astype(jnp.float32) + product[n, rows_of(place)]
        for step in steps:
            arrived(part_recv.at[n, step - 1], part_recv_sem.at[n * 3 + step - 1])
            total = total + part_recv[n, step - 1].astype(jnp.float32)
        spot = pre.at[core, :, n * wide : (n + 1) * wide]
        spot[...] = total.astype(jnp.bfloat16)
        copy = to_core(spot, spot, 2 * PLANE - 1 + n)
        copy.start()
        return copy

    def feed(side, start, stop):
        values = pre[side, :, start * wide : stop * wide].astype(jnp.float32)
        first = pl.multiple_of(side * width + start * wide, wide)
        columns = pl.ds(first, (stop - start) * wide)
        weighed = (values * p_gain_ref[:, columns]).astype(jnp.bfloat16)
        units = jnp.dot(weighed, w_p_in[columns, :], preferred_element_type=jnp.float32)
        return units, jnp.sum(values * values, axis=-1, keepdims=True)

    def add(units, square, more):
        return units + more[0], square + more[1]

    relay(2)
    products(0)
    products(1)
    relay(3)
    products(2)
    pre_copies = [collect(0), collect(1)]
    products(3)
    member_matrix, counts = membership(assign_ref, afeat.shape[0], rows)
    weights[0].wait()
    units, square = feed(core, 0, 2)
    for copy in pre_copies:
        copy.wait()
    units, square = add(units, square, feed(other, 0, 2))
    for n in range(2, chunks):
        copy = collect(n)
        units, square = add(units, square, feed(core, n, n + 1))
        copy.wait()
        units, square = add(units, square, feed(other, n, n + 1))
    hidden = silu(units * lax.rsqrt(square / (2 * width) + epsilon))
    afeat_copy.wait()
    last = 2 * PLANE - 1 + chunks
    after_hidden(
        core,
        hidden,
        member_matrix,
        counts,
        weights,
        to_core,
        (last, last + 1, last + 2),
        afeat,
        afeat_other,
        pre,
        w_p_out,
        w_a_in,
        w_a_out,
        a_gain_ref,
        partial_send,
        partial_recv,
        apart_send,
        apart_recv,
        mid,
        result_ref,
    )

    for n in range(chunks):
        for kind in range(3):
            ring_copy(kind, n).wait_send()
        for step in steps:
            part_copy(n, step).wait_send()
    for step in steps:
        plane_copy(step).wait_send()
        column_copy(step).wait_send()


def direct_kernel(
    count,
    partners_ref,
    tiles_ref,
    feat_ref,
    p_in_hbm,
    p_out_hbm,
    p_gain_ref,
    afeat_ref,
    assign_ref,
    a_in_hbm,
    a_out_hbm,
    a_gain_ref,
    result_ref,
    w_p_in,
    w_p_out,
    w_a_in,
    w_a_out,
    dense,
    back,
    linked,
    mixed,
    pre,
    partial_send,
    partial_recv,
    afeat_other,
    apart_send,
    apart_recv,
    mid,
    w_sem,
    relay_send,
    relay_recv,
    tile_send,
    tile_recv,
    core_send,
    core_recv,
):
    rows, width = feat_ref.shape
    half = rows // 2
    me = lax.axis_index("blk")
    core = lax.axis_index("auth")
    other = 1 - core
    slots = partners_ref.shape[1]

    weights = [
        pltpu.make_async_copy(source, target, w_sem.at[slot])
        for slot, (source, target) in enumerate(
            ((p_in_hbm, w_p_in), (p_out_hbm, w_p_out), (a_in_hbm, w_a_in), (a_out_hbm, w_a_out))
        )
    ]

    barrier = pltpu.get_barrier_semaphore()

    def greet(step, carry):
        block = lax.rem(me + step, count)
        pl.semaphore_signal(barrier, inc=1, device_id={"blk": block}, device_id_type=MESH)
        return carry

    lax.fori_loop(1, count, greet, 0)
    pl.semaphore_signal(barrier, inc=1, device_id={"auth": other}, device_id_type=MESH)

    def fill(block, carry):
        index = jnp.int32(0)
        found = jnp.int32(0)
        for slot in range(slots):
            same = (partners_ref[0, slot] == block).astype(jnp.int32)
            index = jnp.maximum(index, same * slot)
            found = jnp.maximum(found, same)
        tile = tiles_ref[0, index].astype(jnp.float32) * found.astype(jnp.float32)
        tile = tile.astype(jnp.bfloat16)
        dense[0, block] = tile[:half]
        dense[1, block] = tile[half:]
        return carry

    linked[pl.ds(pl.multiple_of(me * rows, rows), rows), :] = feat_ref[...]
    back[core, me] = jnp.zeros((half, rows), jnp.bfloat16)

    pl.semaphore_wait(barrier, count)

    def to_core(source, target, slot):
        return to_other_core(source, target, core_send, core_recv, slot, other)

    def tile_copy(step):
        block = lax.rem(me + step, count)
        return pltpu.make_async_remote_copy(
            src_ref=dense.at[core, block],
            dst_ref=back.at[core, me],
            send_sem=tile_send.at[step],
            recv_sem=tile_recv.at[step],
            device_id={"blk": block},
            device_id_type=MESH,
        )

    afeat_copy = to_core(afeat_ref, afeat_other, 0)
    back_copy = to_core(back.at[core], back.at[core], 1)

    def direct(step):
        return pltpu.make_async_remote_copy(
            src_ref=feat_ref,
            dst_ref=linked.at[pl.ds(pl.multiple_of(me * rows, rows), rows)],
            send_sem=relay_send.at[step],
            recv_sem=relay_recv.at[step],
            device_id={"blk": lax.rem(me + step, count)},
            device_id_type=MESH,
        )

    def run(body):
        def one(step, carry):
            body(step)
            return carry

        lax.fori_loop(1, count, one, 0)

    run(lambda step: direct(step).start())
    lax.fori_loop(0, count, fill, 0)
    run(lambda step: tile_copy(step).start())
    afeat_copy.start()
    for weight in weights:
        weight.start()
    run(lambda step: tile_copy(step).wait())
    back_copy.start()
    back_copy.wait()

    def mix(block, carry):
        own = jnp.concatenate([dense[0, block], dense[1, block]], axis=0)
        came = jnp.concatenate([back[0, block], back[1, block]], axis=0)
        whole = own.astype(jnp.float32) + came.astype(jnp.float32).T
        mixed[:, pl.ds(pl.multiple_of(block * rows, rows), rows)] = whole.astype(jnp.bfloat16)
        return carry

    lax.fori_loop(0, count, mix, 0)
    run(lambda step: direct(step).wait())

    span = min(count * rows, 2048)

    def product(step, total):
        start = pl.multiple_of(step * span, span)
        return total + jnp.dot(
            mixed[:, pl.ds(start, span)],
            linked[pl.ds(start, span), :],
            preferred_element_type=jnp.float32,
        )

    total = feat_ref[...].astype(jnp.float32)
    total = lax.fori_loop(0, count * rows // span, product, total)
    pre[core] = total.astype(jnp.bfloat16)
    pre_copy = to_core(pre.at[core], pre.at[core], 2)
    pre_copy.start()

    member_matrix, counts = membership(assign_ref, afeat_ref.shape[0], rows)
    weights[0].wait()
    own_units, own_square = scaled_units(pre, core, width, p_gain_ref, w_p_in)
    pre_copy.wait()
    far_units, far_square = scaled_units(pre, other, width, p_gain_ref, w_p_in)
    scale = lax.rsqrt((own_square + far_square) / (2 * width) + epsilon)
    hidden = silu((own_units + far_units) * scale)
    afeat_copy.wait()
    after_hidden(
        core,
        hidden,
        member_matrix,
        counts,
        weights,
        to_core,
        (3, 4, 5),
        afeat_ref,
        afeat_other,
        pre,
        w_p_out,
        w_a_in,
        w_a_out,
        a_gain_ref,
        partial_send,
        partial_recv,
        apart_send,
        apart_recv,
        mid,
        result_ref,
    )


def local(
    features,
    partners,
    tiles,
    paper_w_in,
    paper_w_out,
    paper_gain,
    author_feats,
    assign,
    author_w_in,
    author_w_out,
    author_gain,
):
    count = lax.axis_size("blk")
    rows, width = features.shape
    bf16 = jnp.bfloat16
    f32 = jnp.float32
    vmem = pl.BlockSpec(memory_space=pltpu.VMEM)
    hbm = pl.BlockSpec(memory_space=pl.ANY)
    smem = pl.BlockSpec(memory_space=pltpu.SMEM)
    dma = pltpu.SemaphoreType.DMA
    pair = pltpu.VMEM((2, rows, width), bf16)
    single = pltpu.VMEM(author_feats.shape, bf16)
    held = [
        pltpu.VMEM(paper_w_in.shape, bf16),
        pltpu.VMEM(paper_w_out.shape, bf16),
        pltpu.VMEM(author_w_in.shape, bf16),
        pltpu.VMEM(author_w_out.shape, bf16),
    ]
    if count == PLANE * RING and width % LANES == 0:
        chunks = width // LANES
        body = grid_kernel
        near = hbm
        scratch = held + [
            pltpu.VMEM(tiles.shape[1:], bf16),
            pltpu.VMEM((PLANE, rows, RING * rows), bf16),
            pltpu.VMEM((RING, rows, PLANE * rows), bf16),
            pltpu.VMEM((PLANE, rows, RING * rows), bf16),
            pltpu.VMEM((RING, rows, PLANE * rows), bf16),
            pltpu.VMEM((PLANE * rows, RING * rows), bf16),
            pltpu.VMEM((chunks, RING * rows, LANES), bf16),
            pltpu.VMEM((chunks, PLANE * rows, LANES), f32),
            pltpu.VMEM((chunks, PLANE, rows, LANES), bf16),
            pltpu.VMEM((chunks, PLANE - 1, rows, LANES), bf16),
            pair,
            pair,
            pair,
            single,
            single,
            single,
            single,
            pair,
            dma((4,)),
            dma((chunks + 2,)),
            dma((chunks * 3,)),
            dma((chunks * RING,)),
            dma((PLANE + RING,)),
            dma((PLANE + RING,)),
            dma((chunks * (PLANE - 1),)),
            dma((chunks * (PLANE - 1),)),
            dma((2 * PLANE + 2 + chunks,)),
            dma((2 * PLANE + 2 + chunks,)),
        ]
    else:
        body = direct_kernel
        near = vmem
        tile_half = pltpu.VMEM((2, count, rows // 2, rows), bf16)
        scratch = held + [
            tile_half,
            tile_half,
            pltpu.VMEM((count * rows, width), bf16),
            pltpu.VMEM((rows, count * rows), bf16),
            pair,
            pair,
            pair,
            single,
            single,
            single,
            pair,
            dma((4,)),
            dma((count,)),
            dma((count,)),
            dma((count,)),
            dma((count,)),
            dma((6,)),
            dma((6,)),
        ]
    (result,) = pl.pallas_call(
        functools.partial(body, count),
        out_shape=(pltpu.VMEM((2,) + features.shape, bf16),),
        in_specs=[smem, near, near, hbm, hbm, vmem, near, vmem, hbm, hbm, vmem],
        out_specs=(vmem,),
        scratch_shapes=scratch,
        compiler_params=pltpu.CompilerParams(
            collective_id=0, has_side_effects=True, vmem_limit_bytes=56 * 1024 * 1024
        ),
    )(
        partners,
        tiles,
        features,
        paper_w_in,
        paper_w_out,
        paper_gain[None, :],
        author_feats,
        assign[None, :],
        author_w_in,
        author_w_out,
        author_gain[None, :],
    )
    return result[0], result[1]


def solution(mesh):
    placed = (
        P("blk", "auth"),
        P("blk", None),
        P("blk", None, None, None),
        P(None, "auth"),
        P("auth", None),
        P(),
        P("blk", "auth"),
        P("blk"),
        P(None, "auth"),
        P("auth", None),
        P(),
    )
    return jax.shard_map(
        local,
        mesh=mesh,
        in_specs=placed,
        out_specs=(P("blk", "auth"), P("blk", "auth")),
        check_vma=False,
    )
```

time: 38.8 us -> 36.1 us (0.930)
  Pallas kernels: 37.3 us -> 34.6 us
    pallas_call x1, Pallas kernels: 37.3 us -> 34.6 us  [local(): pl.pallas_call(functools.partial(body, count), out_shape=(pltpu.VMEM((2,)...]
where the time goes in v2:
time: 36.1 us; the launch traced here: 36 us
  Pallas kernels  34.6 us (96%)
  local copies, waits for them, and re-layouts  0.72 us (2%)
  between operations  0.64 us (2%)
    pallas_call x1, Pallas kernels, local(): pl.pallas_call(functools.partial(body, count), out_shape=(pltpu.VMEM((2,)...  34.6 us

profile of v2, /device:TPU:0, one launch (start us, length us, event | category | flops | bytes accessed | tf_op | source)
XLA Modules:
  0.0 36.0 jit_solution(1208612595587853767)
XLA Ops:
  0.6 34.6 %shard_map.122 = bf16[2,128,512]{2,1,0:T(8,128)(2,1)S(1)} custom-call(s32[1,8]{1,0:T(1,128)} %partners_ref.1, bf16[1,8,128,128]{3,2,1,0:T(8,128)(2,1)} %tiles_hbm.1, bf16[128,512]{1,0:T(8,128)(2,1)} %feat_hbm.1, bf16[1024,1024]{1,0:T(8,128)(2,1)} %p_in_hbm.1, bf16[1024,1024]{1,0:T(8,128)(2,1)} %p_out_hbm.1, f32[1,1024]{1,0:T(1,128)} %bitcast.7, ...), custom_call_target="tpu_custom_call" | custom-call | tf_op jit(solution)/shard_map/pallas_call | solution.py:724
  35.2 0.7 %slice_bitcast_fusion = (bf16[128,512]{1,0:T(8,128)(2,1)}, bf16[128,512]{1,0:T(8,128)(2,1)}) fusion(bf16[2,128,512]{2,1,0:T(8,128)(2,1)S(1)} %shard_map.122), kind=kLoop, calls=%fused_computation | loop fusion | bytes 524288 | tf_op jit(solution)/shard_map/squeeze | solution.py:746

commit v3 on v2

--- a/solution.py
+++ b/solution.py
@@ -29,11 +29,12 @@
     member = assign_ref[...] == lax.broadcasted_iota(jnp.int32, (authors, rows), 0)
     member_wide = member.astype(jnp.float32)
     counts = jnp.maximum(jnp.sum(member_wide, axis=1, keepdims=True), 1.0)
-    return member_wide.astype(jnp.bfloat16), counts
+    return member_wide.astype(jnp.bfloat16), member_wide.T.astype(jnp.bfloat16), 1.0 / counts
 
 
 def silu(units):
-    return (units / (1.0 + jnp.exp(-units))).astype(jnp.bfloat16)
+    part = 0.5 * units
+    return (part + part * jnp.tanh(part)).astype(jnp.bfloat16)
 
 
 def scaled_units(pre, side, width, p_gain_ref, w_p_in):
@@ -48,12 +49,12 @@
     core,
     hidden,
     member_matrix,
-    counts,
+    member_back,
+    inverse,
     weights,
     to_core,
     slots,
     afeat,
-    afeat_other,
     pre,
     w_p_out,
     w_a_in,
@@ -64,10 +65,11 @@
     apart_send,
     apart_recv,
     mid,
+    author_pre,
     result_ref,
 ):
     other = 1 - core
-    width = afeat.shape[1]
+    width = afeat.shape[2]
     weights[1].wait()
     terms = []
     partial_copies = []
@@ -82,30 +84,23 @@
         copy = to_core(partial_send.at[side], partial_recv.at[side], slots[side])
         copy.start()
         partial_copies.append(copy)
-    author_pre = []
+    terms = [terms[side] + pre[side].astype(jnp.float32) for side in range(2)]
+    weights[2].wait()
+    units = 0.0
+    square = 0.0
     for side in range(2):
+        columns = slice(side * width, (side + 1) * width)
         partial_copies[side].wait()
-        sum_of = pre[side].astype(jnp.float32) + (
-            terms[side] + partial_recv[side].astype(jnp.float32)
-        )
-        mid_side = sum_of.astype(jnp.bfloat16)
+        mid_side = (terms[side] + partial_recv[side].astype(jnp.float32)).astype(jnp.bfloat16)
         mid[side] = mid_side
         author_sum = jnp.dot(member_matrix, mid_side, preferred_element_type=jnp.float32)
-        mine = (core == side).astype(jnp.float32)
-        base = afeat[...].astype(jnp.float32) * mine
-        base = base + afeat_other[...].astype(jnp.float32) * (1.0 - mine)
-        author_pre.append((base + author_sum / counts).astype(jnp.bfloat16))
-    weights[2].wait()
-    left = author_pre[0].astype(jnp.float32)
-    right = author_pre[1].astype(jnp.float32)
-    square = jnp.sum(left * left, axis=-1, keepdims=True)
-    square = square + jnp.sum(right * right, axis=-1, keepdims=True)
-    scale = lax.rsqrt(square / (2 * width) + epsilon)
-    gain = a_gain_ref[...]
-    left = (left * scale * gain[:, :width]).astype(jnp.bfloat16)
-    right = (right * scale * gain[:, width:]).astype(jnp.bfloat16)
-    normed = jnp.concatenate([left, right], axis=1)
-    hidden = silu(jnp.dot(normed, w_a_in[...], preferred_element_type=jnp.float32))
+        whole = (afeat[side].astype(jnp.float32) + author_sum * inverse).astype(jnp.bfloat16)
+        author_pre[side] = whole
+        values = whole.astype(jnp.float32)
+        weighed = (values * a_gain_ref[:, columns]).astype(jnp.bfloat16)
+        units = units + jnp.dot(weighed, w_a_in[columns, :], preferred_element_type=jnp.float32)
+        square = square + jnp.sum(values * values, axis=-1, keepdims=True)
+    hidden = silu(units * lax.rsqrt(square / (2 * width) + epsilon))
     weights[3].wait()
     theirs = pl.ds(pl.multiple_of(other * width, width), width)
     ours = pl.ds(pl.multiple_of(core * width, width), width)
@@ -115,18 +110,11 @@
     apart_copy = to_core(apart_send, apart_recv, slots[2])
     apart_copy.start()
     term = jnp.dot(hidden, w_a_out[:, ours], preferred_element_type=jnp.float32)
-    mine = (core == 0).astype(jnp.float32)
-    own_pre = author_pre[0].astype(jnp.float32) * mine
-    own_pre = own_pre + author_pre[1].astype(jnp.float32) * (1.0 - mine)
+    term = term + author_pre[core].astype(jnp.float32)
     apart_copy.wait()
-    author_out = (own_pre + (term + apart_recv[...].astype(jnp.float32))).astype(jnp.bfloat16)
+    author_out = (term + apart_recv[...].astype(jnp.float32)).astype(jnp.bfloat16)
     result_ref[1] = author_out
-    returned = lax.dot_general(
-        member_matrix,
-        author_out,
-        (((0,), (0,)), ((), ())),
-        preferred_element_type=jnp.float32,
-    )
+    returned = jnp.dot(member_back, author_out, preferred_element_type=jnp.float32)
     result_ref[0] = (mid[core].astype(jnp.float32) + returned).astype(jnp.bfloat16)
 
 
@@ -162,10 +150,10 @@
     partial_send,
     partial_recv,
     afeat,
-    afeat_other,
     apart_send,
     apart_recv,
     mid,
+    author_pre,
     w_sem,
     load_sem,
     ring_send,
@@ -177,7 +165,7 @@
     core_send,
     core_recv,
 ):
-    rows, width = afeat.shape
+    _, rows, width = afeat.shape
     half = rows // 2
     chunks = linked.shape[0]
     wide = width // chunks
@@ -213,7 +201,7 @@
         for n in range(chunks)
     ]
     tile_load = pltpu.make_async_copy(tiles_hbm.at[0], tiles, load_sem.at[chunks])
-    afeat_load = pltpu.make_async_copy(afeat_hbm, afeat, load_sem.at[chunks + 1])
+    afeat_load = pltpu.make_async_copy(afeat_hbm, afeat.at[core], load_sem.at[chunks + 1])
     weights = [
         pltpu.make_async_copy(source, target, w_sem.at[slot])
         for slot, (source, target) in enumerate(
@@ -321,19 +309,21 @@
         upper, inner = block // PLANE, block % PLANE
         ring_tiles[upper, :, inner * rows : (inner + 1) * rows] = tile
         plane_tiles[inner, :, upper * rows : (upper + 1) * rows] = tile
+    start_own(1)
     for step in (2, 1, 3):
         column_copy(step).start()
     for step in (3, 1, 2):
         plane_copy(step).start()
-    start_own(1)
     for weight in weights:
         weight.start()
     afeat_load.wait()
-    afeat_copy = to_core(afeat, afeat_other, 0)
+    afeat_copy = to_core(afeat.at[core], afeat.at[core], 0)
     afeat_copy.start()
 
     relay(0)
     start_own(2)
+    relay(1)
+    start_own(3)
 
     ahead[place] = plane_tiles[place]
     plane_exchange = []
@@ -350,8 +340,6 @@
         copy = to_core(spot, spot, PLANE - 1 + step)
         copy.start()
         column_exchange.append(copy)
-    relay(1)
-    start_own(3)
 
     def mix(origin, came):
         columns = rows_of(origin)
@@ -406,7 +394,7 @@
     products(2)
     pre_copies = [collect(0), collect(1)]
     products(3)
-    member_matrix, counts = membership(assign_ref, afeat.shape[0], rows)
+    member_matrix, member_back, inverse = membership(assign_ref, afeat.shape[1], rows)
     weights[0].wait()
     units, square = feed(core, 0, 2)
     for copy in pre_copies:
@@ -424,12 +412,12 @@
         core,
         hidden,
         member_matrix,
-        counts,
+        member_back,
+        inverse,
         weights,
         to_core,
         (last, last + 1, last + 2),
         afeat,
-        afeat_other,
         pre,
         w_p_out,
         w_a_in,
@@ -440,6 +428,7 @@
         apart_send,
         apart_recv,
         mid,
+        author_pre,
         result_ref,
     )
 
@@ -478,10 +467,11 @@
     pre,
     partial_send,
     partial_recv,
-    afeat_other,
+    afeat,
     apart_send,
     apart_recv,
     mid,
+    author_pre,
     w_sem,
     relay_send,
     relay_recv,
@@ -529,6 +519,7 @@
 
     linked[pl.ds(pl.multiple_of(me * rows, rows), rows), :] = feat_ref[...]
     back[core, me] = jnp.zeros((half, rows), jnp.bfloat16)
+    afeat[core] = afeat_ref[...]
 
     pl.semaphore_wait(barrier, count)
 
@@ -546,7 +537,7 @@
             device_id_type=MESH,
         )
 
-    afeat_copy = to_core(afeat_ref, afeat_other, 0)
+    afeat_copy = to_core(afeat.at[core], afeat.at[core], 0)
     back_copy = to_core(back.at[core], back.at[core], 1)
 
     def direct(step):
@@ -602,7 +593,7 @@
     pre_copy = to_core(pre.at[core], pre.at[core], 2)
     pre_copy.start()
 
-    member_matrix, counts = membership(assign_ref, afeat_ref.shape[0], rows)
+    member_matrix, member_back, inverse = membership(assign_ref, afeat_ref.shape[0], rows)
     weights[0].wait()
     own_units, own_square = scaled_units(pre, core, width, p_gain_ref, w_p_in)
     pre_copy.wait()
@@ -614,12 +605,12 @@
         core,
         hidden,
         member_matrix,
-        counts,
+        member_back,
+        inverse,
         weights,
         to_core,
         (3, 4, 5),
-        afeat_ref,
-        afeat_other,
+        afeat,
         pre,
         w_p_out,
         w_a_in,
@@ -630,6 +621,7 @@
         apart_send,
         apart_recv,
         mid,
+        author_pre,
         result_ref,
     )
 
@@ -681,10 +673,10 @@
             pair,
             pair,
             pair,
+            pair,
             single,
             single,
-            single,
-            single,
+            pair,
             pair,
             dma((4,)),
             dma((chunks + 2,)),
@@ -709,9 +701,10 @@
             pair,
             pair,
             pair,
+            pair,
             single,
             single,
-            single,
+            pair,
             pair,
             dma((4,)),
             dma((count,)),

time: 36.1 us -> 34.7 us (0.961)
  Pallas kernels: 34.6 us -> 33.2 us
    pallas_call x1, Pallas kernels: 34.6 us -> 33.2 us  [local(): pl.pallas_call(functools.partial(body, count), out_shape=(pltpu.VMEM((2,)...]
where the time goes in v3:
time: 34.7 us; the launch traced here: 34.5 us
  Pallas kernels  33.2 us (96%)
  local copies, waits for them, and re-layouts  0.72 us (2%)
  between operations  0.64 us (2%)
    pallas_call x1, Pallas kernels, local(): pl.pallas_call(functools.partial(body, count), out_shape=(pltpu.VMEM((2,)...  33.2 us
    squeeze x1, local copies, waits for them, and re-layouts, local(): return (result[0], result[1])  0.72 us

profile of v3, /device:TPU:0, one launch (start us, length us, event | category | flops | bytes accessed | tf_op | source)
XLA Modules:
  0.0 34.5 jit_solution(9457722783669105203)
XLA Ops:
  0.6 33.2 %shard_map.122 = bf16[2,128,512]{2,1,0:T(8,128)(2,1)S(1)} custom-call(s32[1,8]{1,0:T(1,128)} %partners_ref.1, bf16[1,8,128,128]{3,2,1,0:T(8,128)(2,1)} %tiles_hbm.1, bf16[128,512]{1,0:T(8,128)(2,1)} %feat_hbm.1, bf16[1024,1024]{1,0:T(8,128)(2,1)} %p_in_hbm.1, bf16[1024,1024]{1,0:T(8,128)(2,1)} %p_out_hbm.1, f32[1,1024]{1,0:T(1,128)} %bitcast.7, ...), custom_call_target="tpu_custom_call" | custom-call | tf_op jit(solution)/shard_map/pallas_call | solution.py:717
  33.8 0.7 %slice_bitcast_fusion = (bf16[128,512]{1,0:T(8,128)(2,1)}, bf16[128,512]{1,0:T(8,128)(2,1)}) fusion(bf16[2,128,512]{2,1,0:T(8,128)(2,1)S(1)} %shard_map.122), kind=kLoop, calls=%fused_computation | loop fusion | bytes 524288 | tf_op jit(solution)/shard_map/squeeze | solution.py:739

commit v4 on v3

--- a/solution.py
+++ b/solution.py
@@ -320,8 +320,8 @@
     afeat_copy = to_core(afeat.at[core], afeat.at[core], 0)
     afeat_copy.start()
 
+    start_own(2)
     relay(0)
-    start_own(2)
     relay(1)
     start_own(3)
 
@@ -351,6 +351,7 @@
     for copy in plane_exchange:
         copy.wait()
     mix(z, ring_tiles)
+    relay(2)
     for step in steps:
         column_exchange[step - 1].wait()
         mix(level(RING - step), back)
@@ -387,13 +388,12 @@
     def add(units, square, more):
         return units + more[0], square + more[1]
 
-    relay(2)
     products(0)
     products(1)
     relay(3)
     products(2)
+    products(3)
     pre_copies = [collect(0), collect(1)]
-    products(3)
     member_matrix, member_back, inverse = membership(assign_ref, afeat.shape[1], rows)
     weights[0].wait()
     units, square = feed(core, 0, 2)

time: 34.7 us -> 33.9 us (0.977)
  Pallas kernels: 33.2 us -> 32.4 us
    pallas_call x1, Pallas kernels: 33.2 us -> 32.4 us  [local(): pl.pallas_call(functools.partial(body, count), out_shape=(pltpu.VMEM((2,)...]
where the time goes in v4:
time: 33.9 us; the launch traced here: 33.8 us
  Pallas kernels  32.4 us (96%)
  local copies, waits for them, and re-layouts  0.72 us (2%)
  between operations  0.64 us (2%)
    pallas_call x1, Pallas kernels, local(): pl.pallas_call(functools.partial(body, count), out_shape=(pltpu.VMEM((2,)...  32.4 us
    squeeze x1, local copies, waits for them, and re-layouts, local(): return (result[0], result[1])  0.72 us

profile of v4, /device:TPU:0, one launch (start us, length us, event | category | flops | bytes accessed | tf_op | source)
XLA Modules:
  0.0 33.8 jit_solution(8066927103877927797)
XLA Ops:
  0.6 32.4 %shard_map.122 = bf16[2,128,512]{2,1,0:T(8,128)(2,1)S(1)} custom-call(s32[1,8]{1,0:T(1,128)} %partners_ref.1, bf16[1,8,128,128]{3,2,1,0:T(8,128)(2,1)} %tiles_hbm.1, bf16[128,512]{1,0:T(8,128)(2,1)} %feat_hbm.1, bf16[1024,1024]{1,0:T(8,128)(2,1)} %p_in_hbm.1, bf16[1024,1024]{1,0:T(8,128)(2,1)} %p_out_hbm.1, f32[1,1024]{1,0:T(1,128)} %bitcast.7, ...), custom_call_target="tpu_custom_call" | custom-call | tf_op jit(solution)/shard_map/pallas_call | solution.py:717
  33.1 0.7 %slice_bitcast_fusion = (bf16[128,512]{1,0:T(8,128)(2,1)}, bf16[128,512]{1,0:T(8,128)(2,1)}) fusion(bf16[2,128,512]{2,1,0:T(8,128)(2,1)S(1)} %shard_map.122), kind=kLoop, calls=%fused_computation | loop fusion | bytes 524288 | tf_op jit(solution)/shard_map/squeeze | solution.py:739

commit v5 on v4

--- a/solution.py
+++ b/solution.py
@@ -35,6 +35,19 @@
 def silu(units):
     part = 0.5 * units
     return (part + part * jnp.tanh(part)).astype(jnp.bfloat16)
+
+
+def hidden_of(units, weighed, w_in, columns, scale):
+    span = 2 * LANES
+    parts = []
+    for start in range(0, w_in.shape[1], span):
+        more = jnp.dot(
+            weighed,
+            w_in[columns, start : start + span],
+            preferred_element_type=jnp.float32,
+        )
+        parts.append(silu((units[:, start : start + span] + more) * scale))
+    return jnp.concatenate(parts, axis=1)
 
 
 def scaled_units(pre, side, width, p_gain_ref, w_p_in):
@@ -86,7 +99,6 @@
         partial_copies.append(copy)
     terms = [terms[side] + pre[side].astype(jnp.float32) for side in range(2)]
     weights[2].wait()
-    units = 0.0
     square = 0.0
     for side in range(2):
         columns = slice(side * width, (side + 1) * width)
@@ -98,9 +110,11 @@
         author_pre[side] = whole
         values = whole.astype(jnp.float32)
         weighed = (values * a_gain_ref[:, columns]).astype(jnp.bfloat16)
-        units = units + jnp.dot(weighed, w_a_in[columns, :], preferred_element_type=jnp.float32)
         square = square + jnp.sum(values * values, axis=-1, keepdims=True)
-    hidden = silu(units * lax.rsqrt(square / (2 * width) + epsilon))
+        if side == 0:
+            units = jnp.dot(weighed, w_a_in[columns, :], preferred_element_type=jnp.float32)
+    scale = lax.rsqrt(square / (2 * width) + epsilon)
+    hidden = hidden_of(units, weighed, w_a_in, columns, scale)
     weights[3].wait()
     theirs = pl.ds(pl.multiple_of(other * width, width), width)
     ours = pl.ds(pl.multiple_of(core * width, width), width)
@@ -377,13 +391,17 @@
         copy.start()
         return copy
 
-    def feed(side, start, stop):
+    def weigh(side, start, stop):
         values = pre[side, :, start * wide : stop * wide].astype(jnp.float32)
         first = pl.multiple_of(side * width + start * wide, wide)
         columns = pl.ds(first, (stop - start) * wide)
         weighed = (values * p_gain_ref[:, columns]).astype(jnp.bfloat16)
+        return weighed, columns, jnp.sum(values * values, axis=-1, keepdims=True)
+
+    def feed(side, start, stop):
+        weighed, columns, square = weigh(side, start, stop)
         units = jnp.dot(weighed, w_p_in[columns, :], preferred_element_type=jnp.float32)
-        return units, jnp.sum(values * values, axis=-1, keepdims=True)
+        return units, square
 
     def add(units, square, more):
         return units + more[0], square + more[1]
@@ -404,8 +422,11 @@
         copy = collect(n)
         units, square = add(units, square, feed(core, n, n + 1))
         copy.wait()
-        units, square = add(units, square, feed(other, n, n + 1))
-    hidden = silu(units * lax.rsqrt(square / (2 * width) + epsilon))
+        if n < chunks - 1:
+            units, square = add(units, square, feed(other, n, n + 1))
+    weighed, columns, more = weigh(other, chunks - 1, chunks)
+    scale = lax.rsqrt((square + more) / (2 * width) + epsilon)
+    hidden = hidden_of(units, weighed, w_p_in, columns, scale)
     afeat_copy.wait()
     last = 2 * PLANE - 1 + chunks
     after_hidden(

time: 33.9 us -> 33.8 us (level)
  no operation moved by 1% of the time
where the time goes in v5:
time: 33.8 us; the launch traced here: 33.6 us
  Pallas kernels  32.2 us (95%)
  local copies, waits for them, and re-layouts  0.72 us (2%)
  between operations  0.64 us (2%)
    pallas_call x1, Pallas kernels, local(): pl.pallas_call(functools.partial(body, count), out_shape=(pltpu.VMEM((2,)...  32.2 us
    squeeze x1, local copies, waits for them, and re-layouts, local(): return (result[0], result[1])  0.72 us

profile of v5, /device:TPU:0, one launch (start us, length us, event | category | flops | bytes accessed | tf_op | source)
XLA Modules:
  0.0 33.6 jit_solution(17359288737938543145)
XLA Ops:
  0.6 32.2 %shard_map.122 = bf16[2,128,512]{2,1,0:T(8,128)(2,1)S(1)} custom-call(s32[1,8]{1,0:T(1,128)} %partners_ref.1, bf16[1,8,128,128]{3,2,1,0:T(8,128)(2,1)} %tiles_hbm.1, bf16[128,512]{1,0:T(8,128)(2,1)} %feat_hbm.1, bf16[1024,1024]{1,0:T(8,128)(2,1)} %p_in_hbm.1, bf16[1024,1024]{1,0:T(8,128)(2,1)} %p_out_hbm.1, f32[1,1024]{1,0:T(1,128)} %bitcast.7, ...), custom_call_target="tpu_custom_call" | custom-call | tf_op jit(solution)/shard_map/pallas_call | solution.py:738
  32.9 0.7 %slice_bitcast_fusion = (bf16[128,512]{1,0:T(8,128)(2,1)}, bf16[128,512]{1,0:T(8,128)(2,1)}) fusion(bf16[2,128,512]{2,1,0:T(8,128)(2,1)S(1)} %shard_map.122), kind=kLoop, calls=%fused_computation | loop fusion | bytes 524288 | tf_op jit(solution)/shard_map/squeeze | solution.py:760
